TPU v7x, 16 devices: a whole 2x2x2 slice. The times are simulated.
16 devices in a mesh: dp: 4 (over z, y), ep: 4 (over x, core).
Axes of the slice: x: 2, y: 2, z: 2, core: 2. Of those that a mesh axis runs over, the one named last changes fastest.
Arguments:
- tokens: bfloat16 [4096, 2048], P(('dp', 'ep')), parts along dimension 0
- expert_ids: int32 [4096, 4], P(('dp', 'ep')), parts along dimension 0
- gate_vals: float32 [4096, 4], P(('dp', 'ep')), parts along dimension 0
- w_gate: bfloat16 [60, 2048, 1408], P('ep')
- w_up: bfloat16 [60, 2048, 1408], P('ep')
- w_down: bfloat16 [60, 1408, 2048], P('ep')
- shared_gate: bfloat16 [2048, 5632], replicated
- shared_up: bfloat16 [2048, 5632], replicated
- shared_down: bfloat16 [5632, 2048], replicated
Outputs:
- output: bfloat16 [4096, 2048], P(('dp', 'ep')), parts along dimension 0
There are 4 independent parts. A program takes and returns all parts, laid end to end along the dimension named above; an argument that names none is the same for every part.
All inputs are finite; a program needn't handle non-finite values.
Results may differ from a plain program's by a relative error of at most 0.00670956.
Values are sent between devices in bfloat16 or wider.
A program may use at most 1.25 GiB of HBM per device.

v0:
```python
import jax
import jax.numpy as jnp
from jax import lax
from jax.sharding import PartitionSpec as P


def swiglu(row_block, gate_w, up_w, down_w):
    gate_act = jnp.dot(row_block, gate_w, preferred_element_type=jnp.float32)
    up_act = jnp.dot(row_block, up_w, preferred_element_type=jnp.float32)
    hidden = (jax.nn.silu(gate_act) * up_act).astype(jnp.bfloat16)
    return jnp.dot(hidden, down_w, preferred_element_type=jnp.float32).astype(jnp.bfloat16)


def expert_block(recv_buf, w_gate, w_up, w_down):
    gate_act = jnp.einsum("slcd,ldf->slcf", recv_buf, w_gate, preferred_element_type=jnp.float32)
    up_act = jnp.einsum("slcd,ldf->slcf", recv_buf, w_up, preferred_element_type=jnp.float32)
    hidden = (jax.nn.silu(gate_act) * up_act).astype(jnp.bfloat16)
    return jnp.einsum("slcf,lfd->slcd", hidden, w_down, preferred_element_type=jnp.float32).astype(jnp.bfloat16)


def solution(mesh):
    group_size = mesh.shape["ep"]

    def moe_step(tokens, expert_ids, gate_vals, w_gate, w_up, w_down, shared_gate, shared_up, shared_down):
        tok_count, model_dim = tokens.shape
        top_count = expert_ids.shape[1]
        local_count = w_gate.shape[0]
        expert_count = local_count * group_size
        spread = max(group_size, expert_count // 2)
        capacity = (tok_count * top_count + spread - 1) // spread
        flat_ids = expert_ids.reshape(-1)
        one_hot = (flat_ids[:, None] == jnp.arange(expert_count, dtype=jnp.int32)[None, :]).astype(jnp.int32)
        slot_pos = jnp.sum(jnp.cumsum(one_hot, axis=0) * one_hot, axis=1) - 1
        columns = (flat_ids * capacity + slot_pos).reshape(tok_count, top_count)
        col_range = jnp.arange(expert_count * capacity, dtype=jnp.int32)
        dispatch = jnp.any(columns[:, :, None] == col_range[None, None, :], axis=1).astype(jnp.bfloat16)
        send_buf = jnp.einsum("tn,td->nd", dispatch, tokens, preferred_element_type=jnp.float32).astype(jnp.bfloat16)
        recv_buf = lax.all_to_all(send_buf, "ep", 0, 0, tiled=True)
        expert_out = expert_block(recv_buf.reshape(group_size, local_count, capacity, model_dim), w_gate, w_up, w_down)
        back_buf = lax.all_to_all(expert_out.reshape(expert_count * capacity, model_dim), "ep", 0, 0, tiled=True)
        picked = jnp.take(back_buf, columns, axis=0)
        shared_out = swiglu(tokens, shared_gate, shared_up, shared_down)
        result_acc = tokens.astype(jnp.float32) + jnp.sum(gate_vals[:, :, None] * picked.astype(jnp.float32), axis=1)
        return (result_acc + shared_out.astype(jnp.float32)).astype(jnp.bfloat16)

    row_spec = P(("dp", "ep"), None)
    expert_spec = P("ep", None, None)
    whole_spec = P(None, None)
    return jax.shard_map(moe_step, mesh=mesh, in_specs=(row_spec, row_spec, row_spec, expert_spec, expert_spec, expert_spec, whole_spec, whole_spec, whole_spec), out_specs=row_spec, check_vma=False)
```

profile of v0, /device:TPU:0, one launch (start us, length us, event | category | flops | bytes accessed | tf_op | source)
XLA Modules:
  0.0 445.0 jit_solution(17109171167038556116)
XLA Ops:
  0.0 0.8 copy.50
  0.8 0.1 eq.42
  0.9 0.1 eq.38
  1.1 16.9 %reduce-window.6 = s32[60,8,128]{2,1,0:T(8,128)S(1)} reduce-window(s32[60,8,128]{2,1,0:T(8,128)S(1)} %fusion.22, s32[]{:T(128)} %constant.21.clone.1), window={size=1x1x128 pad=0_0x0_0x127_0}, to_apply=%region_0.0 | reduce-window | flops 7802880 | bytes 491524 | tf_op jit(solution)/shard_map/reduce-window
  18.0 0.1 slice.10
  18.1 0.2 copy.52
  18.3 0.1 copy.53
  18.4 0.1 broadcast_add_fusion
  18.7 0.1 sub.7
  18.9 0.7 compare_and_fusion
  19.6 8.6 %fusion.14 = pred[256,2100]{0,1:T(8,128)(4,1)S(1)} fusion(s32[256,4]{0,1:T(4,128)S(1)} %get-tuple-element.6), kind=kLoop, calls=%fused_computation.19 | loop fusion | flops 3763200 | bytes 541696 | tf_op jit(solution)/shard_map/reduce_or | solution.py:36
  28.2 6.9 %convolution_convert_fusion = bf16[2100,2048]{1,0:T(8,128)(2,1)} fusion(pred[256,2100]{0,1:T(8,128)(4,1)S(1)} %fusion.14, bf16[256,2048]{1,0:T(8,128)(2,1)} %param.9), kind=kOutput, calls=%fused_computation.14 | convolution fusion | flops 2206310400 | bytes 10187776 | tf_op jit(solution)/shard_map/tn,td->nd/dot_general | solution.py:37
  35.1 9.0 %all_to_all.14 = bf16[4,525,2048]{2,1,0:T(8,128)(2,1)} reshape(bf16[2100,2048]{1,0:T(8,128)(2,1)} %convolution_convert_fusion) | data formatting | bytes 17203200 | tf_op jit(solution)/shard_map/all_to_all | solution.py:38
  44.1 100.9 %all_to_all.21 = bf16[4,525,2048]{2,1,0:T(8,128)(2,1)S(1)} all-to-all(bf16[4,525,2048]{2,1,0:T(8,128)(2,1)} %all_to_all.14), channel_id=1, replica_groups=mesh['dp'=4,'ep'=4] {'ep'}, dimensions={0} | all-to-all | bytes 17203200 | tf_op jit(solution)/shard_map/all_to_all | solution.py:38
  145.0 7.7 %copy.56 = bf16[4,525,2048]{2,0,1:T(4,128)(2,1)} copy(bf16[4,525,2048]{2,1,0:T(8,128)(2,1)S(1)} %all_to_all.21) | data formatting | bytes 17203200 | tf_op jit(solution)/shard_map/all_to_all | solution.py:38
  152.7 38.1 %fusion.2 = f32[15,4,35,1408]{3,2,1,0:T(8,128)} fusion(bf16[15,2048,1408]{2,1,0:T(8,128)(2,1)} %param.13, bf16[4,15,35,2048]{3,0,2,1:T(4,128)(2,1)} %bitcast.56), kind=kOutput, calls=%fused_computation.3 | convolution fusion | flops 12111052800 | bytes 106936320 | tf_op jit(solution)/shard_map/slcd,ldf->slcf/dot_general | solution.py:16
  190.8 39.6 %fusion.6 = bf16[4,15,35,1408]{3,2,0,1:T(8,128)(2,1)} fusion(f32[15,4,35,1408]{3,2,1,0:T(8,128)} %fusion.2, bf16[15,2048,1408]{2,1,0:T(8,128)(2,1)} %param.12, bf16[4,15,35,2048]{3,0,2,1:T(4,128)(2,1)} %bitcast.57), kind=kOutput, calls=%fused_computation.8 | convolution fusion | flops 12128796672 | bytes 112849920 | tf_op jit(solution)/shard_map/slcd,ldf->slcf/dot_general | solution.py:15
  230.4 30.6 %convert_bitcast_fusion = bf16[4,15,35,2048]{3,2,0,1:T(8,128)(2,1)S(1)} fusion(bf16[4,15,35,1408]{3,2,0,1:T(8,128)(2,1)} %fusion.6, bf16[15,1408,2048]{2,1,0:T(8,128)(2,1)} %param.14), kind=kOutput, calls=%fused_computation.15 | convolution fusion | flops 12115353600 | bytes 101022720 | tf_op jit(solution)/shard_map/slcf,lfd->slcd/dot_general | solution.py:18
  261.0 9.2 %copy.59 = bf16[4,15,35,2048]{3,0,2,1:T(4,128)(2,1)} copy(bf16[4,15,35,2048]{3,2,0,1:T(8,128)(2,1)S(1)} %convert_bitcast_fusion) | data formatting | bytes 17203200 | tf_op jit(solution)/shard_map/convert_element_type | solution.py:18
  270.2 11.5 %copy.60 = bf16[4,525,2048]{2,1,0:T(8,128)(2,1)} copy(bf16[4,525,2048]{2,0,1:T(4,128)(2,1)} %bitcast.58) | data formatting | bytes 17203200 | tf_op jit(solution)/shard_map/all_to_all | solution.py:40
  281.7 5.8 %all-to-all-start.1 = ((bf16[4,525,2048]{2,1,0:T(8,128)(2,1)}), bf16[4,525,2048]{2,1,0:T(8,128)(2,1)}, u32[]{:S(2)}, u32[]{:S(2)}) async-start(bf16[4,525,2048]{2,1,0:T(8,128)(2,1)} %copy.60), calls=%async_computation.1 | async-start | bytes 17301504 | tf_op jit(solution)/shard_map/all_to_all | solution.py:40
  287.5 0.1 copy.61
  287.7 0.1 reshape.49
  287.8 0.2 copy.55
  288.0 0.1 copy.49
  288.2 13.2 %fusion.24 = f32[256,5632]{1,0:T(8,128)} fusion(bf16[256,2048]{1,0:T(8,128)(2,1)S(1)} %copy-done, bf16[2048,5632]{1,0:T(8,128)(2,1)} %param.15), kind=kOutput, calls=%fused_computation.39 | convolution fusion | flops 5905580032 | bytes 29884416 | tf_op jit(solution)/shard_map/dot_general | solution.py:8
  301.4 81.8 %all-to-all-done.1 = bf16[4,525,2048]{2,1,0:T(8,128)(2,1)} async-done(((bf16[4,525,2048]{2,1,0:T(8,128)(2,1)}), bf16[4,525,2048]{2,1,0:T(8,128)(2,1)}, u32[]{:S(2)}, u32[]{:S(2)}) %all-to-all-start.1) | async-done | bytes 8601632 | tf_op jit(solution)/shard_map/all_to_all | solution.py:40
  383.2 9.0 %all_to_all.18 = bf16[2100,2048]{1,0:T(8,128)(2,1)} reshape(bf16[4,525,2048]{2,1,0:T(8,128)(2,1)} %all-to-all-done.1) | data formatting | bytes 17203200 | tf_op jit(solution)/shard_map/all_to_all | solution.py:40
  392.1 13.4 %gather_fusion = bf16[1024,2048]{1,0:T(8,128)(2,1)} fusion(bf16[2100,2048]{1,0:T(8,128)(2,1)} %all_to_all.18, s32[1024]{0:T(1024)S(1)} %broadcast_clamp_fusion), kind=kCustom, calls=%fused_computation | custom fusion | bytes 8392704 | tf_op jit(solution)/shard_map/jit(_take)/gather | solution.py:41
  405.5 7.2 %reshape.48 = bf16[256,4,2048]{2,1,0:T(4,128)(2,1)} reshape(bf16[1024,2048]{1,0:T(8,128)(2,1)} %gather_fusion) | data formatting | bytes 8388608 | tf_op jit(solution)/shard_map/jit(_take)/gather | solution.py:41
  412.7 9.9 %multiply_reduce_fusion = f32[256,2048]{1,0:T(8,128)S(1)} fusion(bf16[256,4,2048]{2,1,0:T(4,128)(2,1)} %reshape.48, f32[256,4]{1,0:T(8,128)S(1)} %copy.49, pred[256,4]{1,0:T(8,128)(4,1)S(1)} %copy.55), kind=kLoop, calls=%fused_computation.20 | loop fusion | flops 7864320 | bytes 6296576 | tf_op jit(solution)/shard_map/reduce_sum | solution.py:43
  422.7 21.9 %fusion.20 = bf16[256,2048]{1,0:T(8,128)(2,1)} fusion(bf16[5632,2048]{1,0:T(8,128)(2,1)} %param.17, f32[256,2048]{1,0:T(8,128)S(1)} %multiply_reduce_fusion, bf16[256,2048]{1,0:T(8,128)(2,1)S(1)} %copy-done, bf16[2048,5632]{1,0:T(8,128)(2,1)} %param.16, f32[256,5632]{1,0:T(8,128)} %fusion.24), kind=kOutput, calls=%fused_computation.26 | convolution fusion | flops 11822956544 | bytes 56098816 | tf_op jit(solution)/shard_map/dot_general | solution.py:11
  (14 shorter events, 0.3 us)
Async XLA Ops:
  281.7 6.3 %copy-start.1 = (f32[256,4]{0,1:T(4,128)S(1)}, f32[256,4]{0,1:T(4,128)}, u32[]{:S(2)}) copy-start(f32[256,4]{0,1:T(4,128)} %param.11) | copy-start | bytes 12292
  281.7 6.4 %copy-start = (bf16[256,2048]{1,0:T(8,128)(2,1)S(1)}, bf16[256,2048]{1,0:T(8,128)(2,1)}, u32[]{:S(2)}) copy-start(bf16[256,2048]{1,0:T(8,128)(2,1)} %param.9) | copy-start | bytes 3145732
  281.7 101.4 %all-to-all-start.1 = ((bf16[4,525,2048]{2,1,0:T(8,128)(2,1)}), bf16[4,525,2048]{2,1,0:T(8,128)(2,1)}, u32[]{:S(2)}, u32[]{:S(2)}) async-start(bf16[4,525,2048]{2,1,0:T(8,128)(2,1)} %copy.60), calls=%async_computation.1 | async-start | bytes 17301504 | tf_op jit(solution)/shard_map/all_to_all | solution.py:40
where the time goes:
time: 452 us; the launch traced here: 445 us
  matrix products  150 us (33%)
  blocking collectives  101 us (22%)
  waiting for transfers between devices  81.8 us (18%)
  local copies, waits for them, and re-layouts  69.2 us (15%)
  other arithmetic  36.3 us (8%)
  starting transfers between devices  5.81 us (1%)
    all_to_all x1, blocking collectives, moe_step(): recv_buf = lax.all_to_all(send_buf, 'ep', 0, 0, tiled=True)  101 us
    all_to_all x1, waiting for transfers between devices, moe_step(): lax.all_to_all(expert_out.reshape(expert_count * capacity, model_dim), 'e...  81.8 us
    dot_general x1, matrix products, expert_block(): jnp.einsum('slcd,ldf->slcf', recv_buf, w_gate, preferred_element_type=jnp...  39.6 us
    dot_general x1, matrix products, expert_block(): jnp.einsum('slcd,ldf->slcf', recv_buf, w_up, preferred_element_type=jnp.f...  38.1 us
    dot_general x1, matrix products, expert_block(): jnp.einsum('slcf,lfd->slcd', hidden, w_down, preferred_element_type=jnp.f...  30.6 us
    dot_general x1, matrix products, swiglu(): jnp.dot(hidden, down_w, preferred_element_type=jnp.float32)  21.9 us
    gather x2, local copies, waits for them, and re-layouts, moe_step(): picked = jnp.take(back_buf, columns, axis=0)  20.6 us
    all_to_all x2, local copies, waits for them, and re-layouts, moe_step(): lax.all_to_all(expert_out.reshape(expert_count * capacity, model_dim), 'e...  20.5 us
  transfers between devices with their start and end apart: 1, of which 1 were waited for; matrix products, arithmetic and copies ran while one was open for 3% of the time, Pallas kernels for 0%

commit v1 on v0

v1 whole, which is shorter than its diff:
```python
import functools

import jax
import jax.numpy as jnp
from jax import lax
from jax.experimental import pallas as pl
from jax.experimental.pallas import tpu as pltpu
from jax.sharding import PartitionSpec as P

MESH = pl.DeviceIdType.MESH
F32 = jnp.float32
BF16 = jnp.bfloat16

GROUP = 4
CHUNK = 512
SLOTS = 40
EGROUP = 5
RING1 = 3
RING2 = 4
COVER = 2


def dot(a, b):
    return jnp.dot(a, b, preferred_element_type=F32)


def pieces(width):
    return [(start, min(256, width - start)) for start in range(0, width, 256)]


def moe_kernel(dims, ids_ref, gat_ref, tok, w_gate, w_up, w_down, s_gate, s_up, s_down, out,
               ring_g, ring_u, ring_d, acc, sacc, xall, xdf, xd, ybuf, hid, shid, gmat, pmat,
               recv_f, recv_p, recv_q, out_v, meta_loc, meta_all,
               sem_g, sem_u, sem_d, sem_x, sem_o, meta_s, meta_r,
               xq_s, xq_r, xp_s, xp_r, xf_s, xf_r, cf_s, cf_r, cp_s, cp_r, cq_s, cq_r):
    T, D, F, L, NS = dims
    KC = D // CHUNK
    ROWS = GROUP * SLOTS
    NGRP = L // EGROUP
    me = lax.axis_index("ep")
    pp = me + 1 - 2 * lax.rem(me, 2)
    qq = lax.rem(me + 2, GROUP)
    rr = lax.rem(pp + 2, GROUP)

    def remote(src, dst, s_sem, r_sem, dev):
        return pltpu.make_async_remote_copy(src_ref=src, dst_ref=dst, send_sem=s_sem, recv_sem=r_sem,
                                            device_id={"ep": dev}, device_id_type=MESH)

    n_cover = COVER * KC
    n_routed = L * KC
    n_gu = NS * KC + n_routed

    def gu_shared(idx, slot):
        i, k = idx // KC, lax.rem(idx, KC)
        rows, cols = pl.ds(pl.multiple_of(k * CHUNK, CHUNK), CHUNK), pl.ds(pl.multiple_of(i * F, 128), F)
        pltpu.make_async_copy(s_gate.at[rows, cols], ring_g.at[slot], sem_g.at[slot]).start()
        pltpu.make_async_copy(s_up.at[rows, cols], ring_u.at[slot], sem_u.at[slot]).start()

    def issue_gu(g, limit):
        slot = lax.rem(g, RING1)

        @pl.when(jnp.logical_and(g < n_cover, g < limit))
        def _():
            gu_shared(g, slot)

        @pl.when(jnp.logical_and(jnp.logical_and(g >= n_cover, g < n_cover + n_routed), g < limit))
        def _():
            r = g - n_cover
            per = KC * EGROUP
            grp, rest = r // per, lax.rem(r, per)
            k, e = rest // EGROUP, grp * EGROUP + lax.rem(rest, EGROUP)
            rows = pl.ds(pl.multiple_of(k * CHUNK, CHUNK), CHUNK)
            pltpu.make_async_copy(w_gate.at[e, rows, :], ring_g.at[slot], sem_g.at[slot]).start()
            pltpu.make_async_copy(w_up.at[e, rows, :], ring_u.at[slot], sem_u.at[slot]).start()

        @pl.when(jnp.logical_and(g >= n_cover + n_routed, g < limit))
        def _():
            gu_shared(g - n_routed, slot)

    def wait_gu(slot):
        pltpu.make_async_copy(w_gate.at[0, pl.ds(0, CHUNK), :], ring_g.at[slot], sem_g.at[slot]).wait()
        pltpu.make_async_copy(w_up.at[0, pl.ds(0, CHUNK), :], ring_u.at[slot], sem_u.at[slot]).wait()

    n_down = KC * L
    n_dn = n_down + KC * NS

    def issue_dn(t, limit):
        slot = lax.rem(t, RING2)

        @pl.when(jnp.logical_and(t < n_down, t < limit))
        def _():
            n, e = t // L, lax.rem(t, L)
            cols = pl.ds(pl.multiple_of(n * CHUNK, CHUNK), CHUNK)
            pltpu.make_async_copy(w_down.at[e, :, cols], ring_d.at[slot], sem_d.at[slot]).start()

        @pl.when(jnp.logical_and(t >= n_down, t < limit))
        def _():
            n, i = (t - n_down) // NS, lax.rem(t - n_down, NS)
            cols = pl.ds(pl.multiple_of(n * CHUNK, CHUNK), CHUNK)
            rows = pl.ds(pl.multiple_of(i * F, 128), F)
            pltpu.make_async_copy(s_down.at[rows, cols], ring_d.at[slot], sem_d.at[slot]).start()

    def wait_dn(slot):
        pltpu.make_async_copy(w_down.at[0, :, pl.ds(0, CHUNK)], ring_d.at[slot], sem_d.at[slot]).wait()

    def x_load(k):
        return pltpu.make_async_copy(tok.at[:, pl.ds(k * CHUNK, CHUNK)], xall.at[k, me], sem_x.at[k])

    for k in range(KC):
        x_load(k).start()
    for g in range(RING1 - 1):
        issue_gu(jnp.int32(g), n_gu)

    barrier = pltpu.get_barrier_semaphore()
    for dev in (pp, qq, rr):
        pl.semaphore_signal(barrier, inc=1, device_id={"ep": dev}, device_id_type=MESH)

    ids = ids_ref[...]
    gat = gat_ref[...]
    row = lax.broadcasted_iota(jnp.int32, (GROUP * 16, T), 0)
    low = jnp.bitwise_and(row, 15)
    ident = jnp.where(low < L, jnp.right_shift(row, 4) * L + low, -2)
    chosen = jnp.zeros((GROUP * 16, T), F32)
    gates = jnp.zeros((GROUP * 16, T), F32)
    for j in range(4):
        hit = ids[j:j + 1, :] == ident
        chosen = jnp.where(hit, 1.0, chosen)
        gates = jnp.where(hit, gat[j:j + 1, :], gates)
    before = (lax.broadcasted_iota(jnp.int32, (T, T), 0) < lax.broadcasted_iota(jnp.int32, (T, T), 1))
    place = dot(chosen.astype(BF16), jnp.where(before, 1.0, 0.0).astype(BF16))
    place = jnp.where(chosen > 0.5, place, -1.0)
    for d in range(GROUP):
        meta_loc[d, 0:16, :] = place[d * 16:(d + 1) * 16, :]
        meta_loc[d, 16:32, :] = gates[d * 16:(d + 1) * 16, :]

    pl.semaphore_wait(barrier, 3)

    def x_to_q(k, src):
        return remote(xall.at[k, src], xall.at[k, src], xq_s.at[k], xq_r.at[k], qq)

    def x_to_p(k, src):
        return remote(xall.at[k, src], xall.at[k, src], xp_s.at[k], xp_r.at[k], pp)

    def x_fwd(k, src):
        return remote(xall.at[k, src], xall.at[k, src], xf_s.at[k], xf_r.at[k], pp)

    def meta_to(which, dev, src):
        return remote(meta_loc.at[dev], meta_all.at[src], meta_s.at[which], meta_r.at[which], dev)

    for k in range(KC):
        x_load(k).wait()
        x_to_q(k, me).start()
        x_to_p(k, me).start()
    peers = (pp, qq, rr)
    for which, dev in enumerate(peers):
        meta_to(which, dev, me).start()
    meta_all[me] = meta_loc[me]
    ybuf[...] = jnp.zeros(ybuf.shape, F32)

    def silu_mul(g, u):
        return ((g * jax.nn.sigmoid(g)) * u).astype(BF16)

    def gu_step(slot, lhs, acc_ref, row0, rows, k):
        for start, width in pieces(F):
            old_g = acc_ref[pl.ds(row0, rows), pl.ds(start, width)]
            acc_ref[pl.ds(row0, rows), pl.ds(start, width)] = jnp.where(k > 0, old_g, 0.0) + dot(
                lhs, ring_g[slot, :, pl.ds(start, width)])
            old_u = acc_ref[pl.ds(row0, rows), pl.ds(F + start, width)]
            acc_ref[pl.ds(row0, rows), pl.ds(F + start, width)] = jnp.where(k > 0, old_u, 0.0) + dot(
                lhs, ring_u[slot, :, pl.ds(start, width)])

    def shared_gu(idx, g):
        slot = lax.rem(g, RING1)
        i, k = idx // KC, lax.rem(idx, KC)
        wait_gu(slot)
        gu_step(slot, xall[k, me], sacc, 0, T, k)

        @pl.when(k == KC - 1)
        def _():
            for start, width in pieces(F):
                shid[i, :, pl.ds(start, width)] = silu_mul(sacc[:, pl.ds(start, width)], sacc[:, pl.ds(F + start, width)])

    def cover_body(g, carry):
        issue_gu(g + RING1 - 1, n_cover + n_routed)
        shared_gu(g, g)
        return carry

    lax.fori_loop(0, n_cover, cover_body, 0)

    for which, dev in enumerate(peers):
        meta_to(which, dev, dev).wait_recv()

    slot_row = lax.broadcasted_iota(jnp.int32, (SLOTS, T), 0).astype(F32)

    def tables(s, carry):
        for grp in range(NGRP):
            blocks = []
            for j in range(EGROUP):
                e = grp * EGROUP + j
                hit = meta_all[s, e:e + 1, :] == slot_row
                blocks.append(jnp.where(hit, 1.0, 0.0))
                ybuf[0, e * SLOTS:(e + 1) * SLOTS, 0:T] = jnp.where(hit, meta_all[s, 16 + e:17 + e, :], 0.0)
            blocks.append(jnp.zeros((8, T), F32))
            pmat[s, grp] = jnp.concatenate(blocks, axis=0).astype(BF16)
        for start in range(0, 640, 128):
            g = ybuf[0, start:start + 128, 0:T].T
            hi = g.astype(BF16)
            rest = g - hi.astype(F32)
            mid = rest.astype(BF16)
            gmat[0, s, :, start:start + 128] = hi
            gmat[1, s, :, start:start + 128] = mid
            gmat[2, s, :, start:start + 128] = (rest - mid.astype(F32)).astype(BF16)
        return carry

    lax.fori_loop(0, GROUP, tables, 0)

    def routed_body(gk, carry):
        grp, k = gk // KC, lax.rem(gk, KC)

        @pl.when(grp == 0)
        def _():
            x_to_q(k, qq).wait_recv()
            x_fwd(k, qq).start()
            x_to_p(k, pp).wait_recv()
            x_fwd(k, rr).wait_recv()

        @pl.when(gk == NGRP * KC - 1)
        def _():
            for t in range(RING2 - 1):
                issue_dn(jnp.int32(t), n_down)

        for s in range(GROUP):
            lhs = pmat[s, grp]
            for start, width in pieces(CHUNK):
                rows = dot(lhs, xall[k, s, :, pl.ds(start, width)])
                for j in range(EGROUP):
                    xdf[j * ROWS + s * SLOTS:j * ROWS + (s + 1) * SLOTS, pl.ds(start, width)] = rows[j * SLOTS:(j + 1) * SLOTS, :]
        xd[...] = xdf[...].astype(BF16)

        def expert(j, c):
            g = n_cover + gk * EGROUP + j
            issue_gu(g + RING1 - 1, n_cover + n_routed)
            slot = lax.rem(g, RING1)
            wait_gu(slot)
            row0 = pl.multiple_of(j * ROWS, ROWS)
            gu_step(slot, xd[pl.ds(row0, ROWS), :], acc, row0, ROWS, k)

            @pl.when(k == KC - 1)
            def _():
                for start, width in pieces(F):
                    hid[grp * EGROUP + j, :, pl.ds(start, width)] = silu_mul(
                        acc[pl.ds(row0, ROWS), pl.ds(start, width)], acc[pl.ds(row0, ROWS), pl.ds(F + start, width)])
            return c

        lax.fori_loop(0, EGROUP, expert, 0)
        return carry

    lax.fori_loop(0, NGRP * KC, routed_body, 0)
    ybuf[...] = jnp.zeros(ybuf.shape, F32)

    def cf(n):
        return remote(acc.at[pl.ds(0, T), pl.ds(pl.multiple_of(n * CHUNK, CHUNK), CHUNK)], recv_f.at[n], cf_s.at[n], cf_r.at[n], pp)

    def cp(n):
        return remote(acc.at[pl.ds(T, T), pl.ds(pl.multiple_of(n * CHUNK, CHUNK), CHUNK)], recv_p.at[n], cp_s.at[n], cp_r.at[n], pp)

    def cq(n):
        return remote(recv_f.at[n], recv_q.at[n], cq_s.at[n], cq_r.at[n], qq)

    def partial(s, start, width):
        y = ybuf[s, :, pl.ds(start, width)].astype(BF16)
        return dot(gmat[0, s], y) + dot(gmat[1, s], y) + dot(gmat[2, s], y)

    def down_body(n, carry):
        def expert(e, c):
            t = n * L + e
            issue_dn(t + RING2 - 1, n_down)
            slot = lax.rem(t, RING2)
            wait_dn(slot)
            h = hid[e]
            for start, width in pieces(CHUNK):
                y = dot(h, ring_d[slot, :, pl.ds(start, width)]).astype(BF16).astype(F32)
                for s in range(GROUP):
                    ybuf[s, pl.ds(pl.multiple_of(e * SLOTS, 8), SLOTS), pl.ds(start, width)] = y[s * SLOTS:(s + 1) * SLOTS, :]
            return c

        lax.fori_loop(0, L, expert, 0)

        @pl.when(n == KC - 1)
        def _():
            for g in range(RING1 - 1):
                issue_gu(jnp.int32(n_cover + n_routed + g), n_gu)

        col = pl.multiple_of(n * CHUNK, CHUNK)
        for start, width in pieces(CHUNK):
            acc[pl.ds(0, T), pl.ds(col + start, width)] = partial(rr, start, width)
        cf(n).start()
        for start, width in pieces(CHUNK):
            acc[pl.ds(T, T), pl.ds(col + start, width)] = partial(pp, start, width)
        cp(n).start()
        for start, width in pieces(CHUNK):
            acc[pl.ds(2 * T, T), pl.ds(col + start, width)] = partial(me, start, width)
        cf(n).wait_recv()
        for start, width in pieces(CHUNK):
            recv_f[n, :, pl.ds(start, width)] = recv_f[n, :, pl.ds(start, width)] + partial(qq, start, width)
        cq(n).start()
        return carry

    lax.fori_loop(0, KC, down_body, 0)

    for t in range(RING2 - 1):
        issue_dn(jnp.int32(n_down + t), n_dn)

    def rest_body(idx, carry):
        g = n_routed + idx
        issue_gu(g + RING1 - 1, n_gu)
        shared_gu(idx, g)
        return carry

    lax.fori_loop(n_cover, NS * KC, rest_body, 0)

    def shared_down(n, carry):
        col = pl.multiple_of(n * CHUNK, CHUNK)

        def block(i, c):
            t = n_down + n * NS + i
            issue_dn(t + RING2 - 1, n_dn)
            slot = lax.rem(t, RING2)
            wait_dn(slot)
            h = shid[i]
            for start, width in pieces(CHUNK):
                old = sacc[:, pl.ds(start, width)]
                sacc[:, pl.ds(start, width)] = jnp.where(i > 0, old, 0.0) + dot(h, ring_d[slot, :, pl.ds(start, width)])
            return c

        lax.fori_loop(0, NS, block, 0)
        acc[pl.ds(2 * T, T), pl.ds(col, CHUNK)] = acc[pl.ds(2 * T, T), pl.ds(col, CHUNK)] + (
            sacc[:, 0:CHUNK].astype(BF16).astype(F32) + xall[n, me].astype(F32))
        return carry

    lax.fori_loop(0, KC, shared_down, 0)

    def store(n):
        return pltpu.make_async_copy(out_v.at[n], out.at[:, pl.ds(pl.multiple_of(n * CHUNK, CHUNK), CHUNK)], sem_o.at[n])

    def finish(n, carry):
        col = pl.multiple_of(n * CHUNK, CHUNK)
        cp(n).wait_recv()
        cq(n).wait_recv()
        out_v[n] = (acc[pl.ds(2 * T, T), pl.ds(col, CHUNK)] + recv_p[n] + recv_q[n]).astype(BF16)
        store(n).start()
        return carry

    lax.fori_loop(0, KC, finish, 0)

    for k in range(KC):
        x_to_q(k, me).wait_send()
        x_to_p(k, me).wait_send()
        x_fwd(k, qq).wait_send()
        cf(k).wait_send()
        cp(k).wait_send()
        cq(k).wait_send()
        store(k).wait()
    for which, dev in enumerate(peers):
        meta_to(which, dev, me).wait_send()


def solution(mesh):
    assert mesh.shape["ep"] == GROUP

    def moe_step(tokens, expert_ids, gate_vals, w_gate, w_up, w_down, shared_gate, shared_up, shared_down):
        T, D = tokens.shape
        L, _, F = w_gate.shape
        NS = shared_gate.shape[1] // F
        KC = D // CHUNK
        ROWS = GROUP * SLOTS
        top = expert_ids.shape[1]
        ids_t = jnp.pad(expert_ids.T, ((0, 8 - top), (0, 0)), constant_values=-1)
        gat_t = jnp.pad(gate_vals.T, ((0, 8 - top), (0, 0)))
        vmem = pl.BlockSpec(memory_space=pltpu.VMEM)
        hbm = pl.BlockSpec(memory_space=pl.ANY)
        dma = pltpu.SemaphoreType.DMA
        return pl.pallas_call(
            functools.partial(moe_kernel, (T, D, F, L, NS)),
            out_shape=jax.ShapeDtypeStruct((T, D), BF16),
            in_specs=[vmem, vmem] + [hbm] * 7,
            out_specs=hbm,
            scratch_shapes=[
                pltpu.VMEM((RING1, CHUNK, F), BF16),
                pltpu.VMEM((RING1, CHUNK, F), BF16),
                pltpu.VMEM((RING2, F, CHUNK), BF16),
                pltpu.VMEM((EGROUP * ROWS, 2 * F), F32),
                pltpu.VMEM((T, 2 * F), F32),
                pltpu.VMEM((KC, GROUP, T, CHUNK), BF16),
                pltpu.VMEM((EGROUP * ROWS, CHUNK), F32),
                pltpu.VMEM((EGROUP * ROWS, CHUNK), BF16),
                pltpu.VMEM((GROUP, 640, CHUNK), F32),
                pltpu.VMEM((L, ROWS, F), BF16),
                pltpu.VMEM((NS, T, F), BF16),
                pltpu.VMEM((3, GROUP, T, 640), BF16),
                pltpu.VMEM((GROUP, L // EGROUP, EGROUP * SLOTS + 8, T), BF16),
                pltpu.VMEM((KC, T, CHUNK), F32),
                pltpu.VMEM((KC, T, CHUNK), F32),
                pltpu.VMEM((KC, T, CHUNK), F32),
                pltpu.VMEM((KC, T, CHUNK), BF16),
                pltpu.VMEM((GROUP, 32, T), F32),
                pltpu.VMEM((GROUP, 32, T), F32),
                dma((RING1,)), dma((RING1,)), dma((RING2,)), dma((KC,)), dma((KC,)), dma((3,)), dma((3,)),
                dma((KC,)), dma((KC,)), dma((KC,)), dma((KC,)), dma((KC,)), dma((KC,)),
                dma((KC,)), dma((KC,)), dma((KC,)), dma((KC,)), dma((KC,)), dma((KC,)),
            ],
            compiler_params=pltpu.CompilerParams(
                collective_id=0, has_side_effects=True, vmem_limit_bytes=67043328),
        )(ids_t, gat_t, tokens, w_gate, w_up, w_down, shared_gate, shared_up, shared_down)

    row_spec = P(("dp", "ep"), None)
    expert_spec = P("ep", None, None)
    whole_spec = P(None, None)
    return jax.shard_map(moe_step, mesh=mesh, in_specs=(row_spec, row_spec, row_spec, expert_spec, expert_spec, expert_spec, whole_spec, whole_spec, whole_spec), out_specs=row_spec, check_vma=False)
```

time: 452 us -> 164 us (0.36); the launches traced: 445 us -> 164 us
  Pallas kernels: 0 us -> 159 us
  matrix products: 150 us -> 0 us
  blocking collectives: 101 us -> 0 us
  waiting for transfers between devices: 81.8 us -> 0 us
  local copies, waits for them, and re-layouts: 69.2 us -> 4.87 us
  other arithmetic: 36.3 us -> 0 us
  starting transfers between devices: 5.81 us -> 0 us
    pallas_call x0 -> x1, Pallas kernels: none -> 159 us  [moe_step(): pl.pallas_call(functools.partial(moe_kernel, (T, D, F, L, NS)), out_shape...]
    dot_general x6 -> x0, matrix products: 150 us -> none  [the longest x1 39.6 us: expert_block(): jnp.einsum('slcd,ldf->slcf', recv_buf, w_gate, preferred_element_type=jnp...]
    all_to_all x1 -> x0, blocking collectives: 101 us -> none  [moe_step(): recv_buf = lax.all_to_all(send_buf, 'ep', 0, 0, tiled=True)]
    all_to_all x1 -> x0, waiting for transfers between devices: 81.8 us -> none  [moe_step(): lax.all_to_all(expert_out.reshape(expert_count * capacity, model_dim), 'e...]
    all_to_all x4 -> x0, local copies, waits for them, and re-layouts: 37.2 us -> none  [the longest x2 20.5 us: moe_step(): lax.all_to_all(expert_out.reshape(expert_count * capacity, model_dim), 'e...]
    gather x2 -> x0, local copies, waits for them, and re-layouts: 20.6 us -> none  [moe_step(): picked = jnp.take(back_buf, columns, axis=0)]
    another operation x3 -> x0, other arithmetic: 17 us -> none
    reduce_sum x2 -> x0, other arithmetic: 9.99 us -> none  [the longest x1 9.95 us: moe_step(): jnp.sum(gate_vals[:, :, None] * picked.astype(jnp.float32), axis=1)]
  transfers between devices with their start and end apart: 1 -> 0, of which waited for: 1 -> 0; matrix products, arithmetic and copies ran while one was open for 3% -> 0% of each run, Pallas kernels for 0% -> 0%
where the time goes in v1:
time: 164 us
  Pallas kernels  159 us (97%)
  local copies, waits for them, and re-layouts  4.87 us (3%)
    pallas_call x1, Pallas kernels, moe_step(): pl.pallas_call(functools.partial(moe_kernel, (T, D, F, L, NS)), out_shape...  159 us

profile of v1, /device:TPU:0, one launch (start us, length us, event | category | flops | bytes accessed | tf_op | source)
XLA Modules:
  0.0 163.7 jit_solution(10481040050841998850)
XLA Ops:
  0.0 1.3 pad.8.ids_ref
  1.3 1.3 pad.9.gat_ref
  2.6 158.9 %shard_map.91 = bf16[256,2048]{1,0:T(8,128)(2,1)} custom-call(s32[8,256]{1,0:T(8,128)} %pad.8.ids_ref, f32[8,256]{1,0:T(8,128)} %pad.9.gat_ref, bf16[256,2048]{1,0:T(8,128)(2,1)} %tok.1, bf16[15,2048,1408]{2,1,0:T(8,128)(2,1)} %w_gate.1, bf16[15,2048,1408]{2,1,0:T(8,128)(2,1)} %w_up.1, bf16[15,1408,2048]{2,1,0:T(8,128)(2,1)} %w_down.1, ...), custom_call_target="tpu_custom_call" | custom-call | tf_op jit(solution)/shard_map/pallas_call | solution.py:383
  161.4 2.3 %copy.11 = bf16[256,2048]{1,0:T(8,128)(2,1)} copy(bf16[256,2048]{1,0:T(8,128)(2,1)} %shard_map.91) | data formatting | bytes 2097152
